TPU v7x, 32 devices: a whole 2x2x4 slice. The times are simulated.
32 devices in a mesh: gx: 16 (over z, y, x), gy: 2 (over core).
Axes of the slice: x: 2, y: 2, z: 4, core: 2. Of those that a mesh axis runs over, the one named last changes fastest.
Arguments:
- droplets: float32 [2, 32, 32, 1024], P(None, None, 'gx', 'gy'), as said below
- moves: int32 [2, 32, 32, 1024], P(None, None, 'gx', 'gy'), may hold values from 0 to 8, as said below
- pairing: int32 [2, 32, 32, 1024], P(None, None, 'gx', 'gy'), may hold values from 0 to 31, as said below
- collisions: int32 [2, 16, 32, 1024], P(None, None, 'gx', 'gy'), may hold values from 0 to 3
Outputs:
- droplets_out: float32 [2, 32, 32, 1024], P(None, None, 'gx', 'gy')
- moments: float32 [2, 2, 16], replicated
Inputs may be any that keep to these rules, and one draw needn't show every extreme that they name: `droplets`: entry 0 holds whole-number multiplicities from 24 to below 300, entry 1 masses from 0.05 to 2. `moves`: A code c means a step of c // 3 - 1 along x and c % 3 - 1 along y. In each step, slot and level, all droplets of one y-row take the same x-step and all droplets landing in one x-column take the same y-step, so every cell and slot receives exactly one droplet. `pairing`: for each step and cell, the entries along the slot dimension are a permutation of 0 to 31.
All inputs are finite; a program needn't handle non-finite values.
Results may differ from a plain program's by a relative error of at most 0.0003.
Values sent between devices are 32-bit elements; how exact they have to be, the bound alone decides.
A program may use at most 64 MiB of HBM per device.

v0:
```python
import jax
import jax.numpy as jnp
from jax import lax
from jax.sharding import PartitionSpec as P

LEVELS = 16
count_unit = 4096.0


def padded(array, sides, width):
    for axis, dim in sides:
        size, length = (lax.axis_size(axis), array.shape[dim])
        up = [(i, (i + 1) % size) for i in range(size)]
        down = [(j, i) for i, j in up]
        last = lax.slice_in_dim(array, length - width, length, axis=dim)
        leading = lax.slice_in_dim(array, 0, width, axis=dim)
        before = lax.ppermute(last, axis, up)
        after = lax.ppermute(leading, axis, down)
        array = jnp.concatenate([before, array, after], axis=dim)
    return array


def spread(state, codes):
    twos, slots, cols, rows, levels = state.shape
    extended = jnp.zeros((twos, slots, cols + 2, rows + 2, levels), state.dtype)
    for direction in range(9):
        step_x = direction // 3 - 1
        step_y = direction % 3 - 1
        chosen = jnp.where((codes == direction)[None], state, jnp.zeros_like(state))
        extended = extended + jnp.pad(
            chosen, ((0, 0), (0, 0), (1 + step_x, 1 - step_x), (1 + step_y, 1 - step_y), (0, 0))
        )
    return extended


def settle(extended, cols, rows):
    twos, slots, wide, tall, levels = extended.shape
    rims = jnp.stack([extended[:, :, 0], extended[:, :, cols + 1]], axis=2).reshape(
        twos, slots, 2, (rows + 2) * levels
    )
    got = padded(rims, (("gx", 2),), 1).reshape(twos, slots, 4, rows + 2, levels)
    middle = (
        extended[:, :, 1 : cols + 1]
        .at[:, :, 0]
        .add(got[:, :, 0])
        .at[:, :, cols - 1]
        .add(got[:, :, 3])
    )
    rims = jnp.stack([middle[:, :, :, 0], middle[:, :, :, rows + 1]], axis=2).reshape(
        twos, slots, 2, cols * levels
    )
    got = padded(rims, (("gy", 2),), 1).reshape(twos, slots, 4, cols, levels)
    block = (
        middle[:, :, :, 1 : rows + 1]
        .at[:, :, :, 0]
        .add(got[:, :, 0])
        .at[:, :, :, rows - 1]
        .add(got[:, :, 3])
    )
    return block


def collide(first_count, second_count, first_mass, second_mass, tries):
    big_first = first_count >= second_count
    larger = jnp.where(big_first, first_count, second_count)
    smaller = jnp.where(big_first, second_count, first_count)
    larger_mass = jnp.where(big_first, first_mass, second_mass)
    smaller_mass = jnp.where(big_first, second_mass, first_mass)
    taken = jnp.minimum(tries, larger // smaller)
    remain = larger - taken * smaller
    splits = remain == 0
    halved = smaller // 2
    larger_new = jnp.where(splits, halved, remain)
    smaller_new = jnp.where(splits, smaller - halved, smaller)
    grown = smaller_mass + taken.astype(first_mass.dtype) * larger_mass
    larger_mass_new = jnp.where(splits, grown, larger_mass)
    first_new = jnp.where(big_first, larger_new, smaller_new)
    second_new = jnp.where(big_first, smaller_new, larger_new)
    first_mass_new = jnp.where(big_first, larger_mass_new, grown)
    second_mass_new = jnp.where(big_first, grown, larger_mass_new)
    return (first_new, second_new, first_mass_new, second_mass_new)


def pair_column(counts_f, masses, order, tries):
    slots = counts_f.shape[0]
    slot_ids = lax.broadcasted_iota(jnp.int32, (slots, slots, 1), 1)
    hits = order[:, None, :] == slot_ids
    counts = counts_f.astype(jnp.int32)
    counts_p = jnp.sum(jnp.where(hits, counts[None], 0), axis=1)
    masses_p = jnp.sum(jnp.where(hits, masses[None], jnp.zeros_like(masses)[None]), axis=1)
    first_new, second_new, first_mass, second_mass = collide(
        counts_p[0::2], counts_p[1::2], masses_p[0::2], masses_p[1::2], tries
    )
    counts_pair = jnp.stack([first_new, second_new], axis=1).reshape(counts_p.shape)
    masses_pair = jnp.stack([first_mass, second_mass], axis=1).reshape(masses_p.shape)
    counts_new = jnp.sum(jnp.where(hits, counts_pair[:, None], 0), axis=0)
    masses_new = jnp.sum(
        jnp.where(hits, masses_pair[:, None], jnp.zeros_like(masses_pair)[:, None]), axis=0
    )
    return (counts_new.astype(counts_f.dtype), masses_new)


def coalesce(block, order, tries):
    twos, slots, cols, rows, levels = block.shape
    flat = block.reshape(twos, slots, cols, rows * levels)
    results = []
    for column in range(cols):
        counts_new, masses_new = pair_column(
            flat[0, :, column], flat[1, :, column], order[:, column], tries[:, column]
        )
        results.append(jnp.stack([counts_new, masses_new]))
    return jnp.stack(results, axis=2).reshape(block.shape)


def shards(droplets, moves, pairing, collisions):
    twos, slots, cols, flat = droplets.shape
    levels = LEVELS
    rows = flat // levels
    state = droplets.reshape(twos, slots, cols, rows, levels)
    totals = []
    for step in range(moves.shape[0]):
        codes = moves[step].reshape(slots, cols, rows, levels)
        state = settle(spread(state, codes), cols, rows)
        state = coalesce(state, pairing[step], collisions[step])
        count_sum = jnp.sum(state[0], axis=(0, 1, 2))
        liquid_sum = jnp.sum(state[0] * state[1], axis=(0, 1, 2))
        terms = jnp.stack([count_sum, liquid_sum])
        totals.append(lax.psum(terms, ("gx", "gy")))
    summed = jnp.stack(totals)
    cells_x = cols * lax.axis_size("gx")
    cells_y = rows * lax.axis_size("gy")
    moments = summed / (cells_x * cells_y * count_unit)
    return (state.reshape(droplets.shape), moments)


def solution(mesh):
    placed = (
        P(None, None, "gx", "gy"),
        P(None, None, "gx", "gy"),
        P(None, None, "gx", "gy"),
        P(None, None, "gx", "gy"),
    )
    return jax.shard_map(
        shards,
        mesh=mesh,
        in_specs=placed,
        out_specs=(P(None, None, "gx", "gy"), P()),
        check_vma=False,
    )
```

profile of v0, /device:TPU:0, one launch (start us, length us, event | category | flops | bytes accessed | tf_op | source)
XLA Modules:
  0.0 107.8 jit_solution(15676673924151060772)
XLA Ops:
  0.6 1.0 fusion.55
  1.9 0.8 broadcast_compare_fusion.16
  3.1 1.2 %broadcast_select_fusion.17 = (f32[2,32,2,32,16]{1,4,3,2,0:T(8,128)S(1)}, f32[2,32,2,32,16]{1,4,3,2,0:T(8,128)S(1)}, f32[2,32,2,32,16]{1,4,3,2,0:T(8,128)S(1)}, ...) fusion(f32[2,32,2,32,16]{1,4,3,2,0:T(8,128)S(1)} %bitcast.219, ...), kind=kLoop, calls=%fused_computation.50 | loop fusion | flops 589824 | bytes 2916352 | tf_op jit(solution)/shard_map/jit(_where)/select_n | solution.py:29
  4.3 0.6 pad_add_fusion.1
  5.2 1.1 %copy.85 = f32[2,32,1,544]{3,1,2,0:T(8,128)} copy(f32[2,32,1,544]{1,3,2,0:T(8,128)S(1)} %get-tuple-element.121) | data formatting | bytes 278528 | tf_op jit(solution)/shard_map/slice | solution.py:15
  6.3 3.0 %collective-permute-start = (f32[2,32,1,544]{3,1,2,0:T(8,128)}, f32[2,32,1,544]{3,1,2,0:T(8,128)}, u32[]{:S(2)}, u32[]{:S(2)}) collective-permute-start(f32[2,32,1,544]{3,1,2,0:T(8,128)} %copy.85), channel_id=1, source_target_pairs={{0,2},{2,4},{4,6},{6,8},{8,10},{10,12},{12,14},{14,16},{16,18},{18... | collective-permute-start | bytes 417800 | tf_op jit(solution)/shard_map/ppermute | solution.py:17
  9.2 0.9 copy.88
  10.1 4.0 %collective-permute-start.1 = (f32[2,32,1,544]{3,1,2,0:T(8,128)}, f32[2,32,1,544]{3,1,2,0:T(8,128)}, u32[]{:S(2)}, u32[]{:S(2)}) collective-permute-start(f32[2,32,1,544]{3,1,2,0:T(8,128)} %copy.88), channel_id=1, source_target_pairs={{2,0},{4,2},{6,4},{8,6},{10,8},{12,10},{14,12},{16,14},{18,16},{20... | collective-permute-start | bytes 417800 | tf_op jit(solution)/shard_map/ppermute | solution.py:18
  14.1 0.7 slice_bitcast_fusion.5
  14.8 1.0 copy.130
  15.9 2.5 %broadcast_compare_fusion.17 = (pred[1,32,2,512]{1,3,2,0:T(8,128)(4,1)}, pred[1,32,2,512]{1,3,2,0:T(8,128)(4,1)}, pred[1,32,2,512]{1,3,2,0:T(8,128)(4,1)}, pred[...) fusion(s32[1,32,2,512]{1,3,2,0:T(8,128)} %copy.130), kind=kLoop, calls=%fused_computation.87 | loop fusion | flops 294912 | bytes 425984 | tf_op jit(solution)/shard_map/eq | solution.py:29
  18.4 2.0 %fusion.56 = (s32[32,1,512]{2,1,0:T(1,128)}, s32[32,1,512]{2,1,0:T(1,128)}, s32[32,1,512]{2,1,0:T(1,128)}, s32[32,1,512]{2,1,0:T(1,128)}) fusion(s32[32,2,512]{2,1,0:T(2,128)} %get-tuple-element.166, s32[32,2,512]{2,1,0:T(2,128)} %get-tuple-element.167), kind=kLoop, calls=%fused_computation.232 | loop fusion | bytes 524288 | tf_op jit(solution)/shard_map/slice | solution.py:109
  20.4 0.9 fusion.57
  21.3 1.9 %copy.86 = f32[2,32,1,544]{1,3,0,2:T(8,128)} copy(f32[2,32,1,544]{3,1,2,0:T(8,128)} %collective-permute-done) | data formatting | bytes 278528 | tf_op jit(solution)/shard_map/ppermute | solution.py:17
  23.3 1.1 %fusion.3 = f32[2,32,2,34,16]{1,4,3,2,0:T(8,128)S(1)} fusion(f32[2,32,2,34,16]{1,4,3,2,0:T(8,128)S(1)} %slice-done, f32[2,32,1,34,16]{1,4,3,2,0:T(8,128)} %bitcast.220, f32[2,32,4,34,16]{1,4,3,2,0:T(8,128)S(1)} %copy-done.1), kind=kLoop, calls=%fused_computation.32 | loop fusion | flops 34816 | bytes 1253376 | tf_op jit(solution)/shard_map/scatter-add | solution.py:45
  24.4 1.2 %copy.89 = f32[2,32,1,544]{1,3,0,2:T(8,128)S(1)} copy(f32[2,32,1,544]{3,1,2,0:T(8,128)} %collective-permute-done.1) | data formatting | bytes 278528 | tf_op jit(solution)/shard_map/ppermute | solution.py:18
  26.1 0.6 collective-permute-start.3
  26.7 0.4 collective-permute-done.2
  27.1 0.5 collective-permute-done.3
  27.7 0.4 select_reduce_fusion.11
  28.3 0.4 select_reduce_fusion.15
  28.9 0.4 select_reduce_fusion.9
  29.4 0.4 select_reduce_fusion.13
  29.9 0.8 select_bitcast_fusion.7
  30.8 0.4 select_reduce_fusion.14
  31.2 0.6 convert_bitcast_fusion.3
  31.8 0.7 fusion.15
  32.7 0.4 select_reduce_fusion.12
  33.2 0.4 select_reduce_fusion.10
  33.5 0.6 convert_bitcast_fusion.2
  34.3 0.4 select_reduce_fusion.8
  35.2 0.3 broadcast_select_fusion.8
  35.6 0.5 copy-done.6
  36.6 0.5 copy-done.3
  37.6 0.6 pad_add_fusion
  38.5 0.9 fusion.52
  39.3 0.9 copy.106
  40.3 0.9 maximum_bitcast_fusion.3
  41.2 0.6 fusion.48
  41.8 0.8 reduce_sum.225
  42.6 1.4 %reduce_sum.228 = f32[32,16]{1,0:T(8,128)} reshape(f32[512]{0:T(512)} %get-tuple-element.105) | data formatting | bytes 4096 | tf_op jit(solution)/shard_map/reduce_sum | solution.py:126
  43.9 0.5 reduce_sum.226
  44.5 0.7 reduce_sum.229
  45.2 1.9 %copy.109 = f32[2,32,1,544]{3,1,2,0:T(8,128)} copy(f32[2,32,1,544]{1,3,2,0:T(8,128)} %get-tuple-element.116) | data formatting | bytes 278528 | tf_op jit(solution)/shard_map/slice | solution.py:16
  47.1 5.6 %collective-permute-start.5 = (f32[2,32,1,544]{3,1,2,0:T(8,128)}, f32[2,32,1,544]{3,1,2,0:T(8,128)}, u32[]{:S(2)}, u32[]{:S(2)}) collective-permute-start(f32[2,32,1,544]{3,1,2,0:T(8,128)} %copy.109), channel_id=1, source_target_pairs={{2,0},{4,2},{6,4},{8,6},{10,8},{12,10},{14,12},{16,14},{18,16},{20... | collective-permute-start | bytes 417800 | tf_op jit(solution)/shard_map/ppermute | solution.py:18
  52.7 1.9 %copy.107 = f32[2,32,1,544]{1,3,0,2:T(8,128)} copy(f32[2,32,1,544]{3,1,2,0:T(8,128)} %collective-permute-done.4) | data formatting | bytes 278528 | tf_op jit(solution)/shard_map/ppermute | solution.py:17
  54.6 1.1 %fusion.1 = f32[2,32,2,34,16]{1,4,3,2,0:T(8,128)S(1)} fusion(f32[2,32,2,34,16]{1,4,3,2,0:T(8,128)S(1)} %slice.539, f32[2,32,1,34,16]{1,4,3,2,0:T(8,128)} %bitcast.221, f32[2,32,4,34,16]{1,4,3,2,0:T(8,128)S(1)} %pad_add_fusion), kind=kLoop, calls=%fused_computation.28 | loop fusion | flops 34816 | bytes 1253376 | tf_op jit(solution)/shard_map/scatter-add | solution.py:45
  55.8 1.0 collective-permute-done.5
  56.7 1.1 %copy.110 = f32[2,32,1,544]{1,3,0,2:T(8,128)S(1)} copy(f32[2,32,1,544]{3,1,2,0:T(8,128)} %collective-permute-done.5) | data formatting | bytes 278528 | tf_op jit(solution)/shard_map/ppermute | solution.py:18
  58.2 0.5 collective-permute-start.7
  58.8 0.5 collective-permute-done.6
  59.8 0.4 select_reduce_fusion.3
  60.4 0.4 select_reduce_fusion.7
  61.0 0.4 select_reduce_fusion.1
  61.6 0.4 select_reduce_fusion.5
  62.0 0.8 select_bitcast_fusion.3
  62.9 0.4 select_reduce_fusion.6
  63.3 0.7 fusion.19
  64.2 0.4 select_reduce_fusion.4
  64.7 0.4 select_reduce_fusion.2
  65.2 0.4 select_reduce_fusion
  65.8 0.9 copy.125
  66.8 40.4 %all-reduce.18 = (f32[1,2,16]{2,1,0:T(2,128)S(1)}, f32[1,2,16]{2,1,0:T(2,128)S(1)}) all-reduce(f32[1,2,16]{2,1,0:T(2,128)S(1)} %maximum_bitcast_fusion.5, f32[1,2,16]{2,1,0:T(2,128)S(1)} %maximum_bitcast_fusion.4), channel_id=1, replica_groups=mesh['gx'=16,'gy'=2] {'gx','gy'}, use_global_device_ids=true, to_apply=%region_25.26 | all-reduce | flops 64 | bytes 512 | tf_op jit(solution)/shard_map/psum | solution.py:128
  107.2 0.6 maximum_multiply_fusion
  (139 shorter events, 6.1 us)
Async XLA Ops:
  0.6 2.1 %copy-start.12 = (f32[2,32,2,512]{3,2,1,0:T(2,128)S(1)}, f32[2,32,2,512]{3,2,1,0:T(2,128)}, u32[]{:S(2)}) copy-start(f32[2,32,2,512]{3,2,1,0:T(2,128)} %param.20) | copy-start | bytes 786436
  4.9 9.2 %copy-start = (f32[2,32,4,34,16]{1,4,3,2,0:T(8,128)}, f32[2,32,4,34,16]{1,4,3,2,0:T(8,128)S(1)}, u32[]{:S(2)}) copy-start(f32[2,32,4,34,16]{1,4,3,2,0:T(8,128)S(1)} %pad_add_fusion.1) | copy-start | bytes 1671172
  6.3 15.0 %collective-permute-start = (f32[2,32,1,544]{3,1,2,0:T(8,128)}, f32[2,32,1,544]{3,1,2,0:T(8,128)}, u32[]{:S(2)}, u32[]{:S(2)}) collective-permute-start(f32[2,32,1,544]{3,1,2,0:T(8,128)} %copy.85), channel_id=1, source_target_pairs={{0,2},{2,4},{4,6},{6,8},{8,10},{10,12},{12,14},{14,16},{16,18},{18... | collective-permute-start | bytes 417800 | tf_op jit(solution)/shard_map/ppermute | solution.py:17
  10.1 4.0 %copy-start.13 = (s32[2,32,2,512]{3,2,1,0:T(2,128)S(1)}, s32[2,32,2,512]{3,2,1,0:T(2,128)}, u32[]{:S(2)}) copy-start(s32[2,32,2,512]{3,2,1,0:T(2,128)} %param.22) | copy-start | bytes 786436
  10.1 14.3 %collective-permute-start.1 = (f32[2,32,1,544]{3,1,2,0:T(8,128)}, f32[2,32,1,544]{3,1,2,0:T(8,128)}, u32[]{:S(2)}, u32[]{:S(2)}) collective-permute-start(f32[2,32,1,544]{3,1,2,0:T(8,128)} %copy.88), channel_id=1, source_target_pairs={{2,0},{4,2},{6,4},{8,6},{10,8},{12,10},{14,12},{16,14},{18,16},{20... | collective-permute-start | bytes 417800 | tf_op jit(solution)/shard_map/ppermute | solution.py:18
  14.1 9.1 %copy-start.1 = (f32[2,32,4,34,16]{1,4,3,2,0:T(8,128)S(1)}, f32[2,32,4,34,16]{1,4,3,2,0:T(8,128)}, u32[]{:S(2)}) copy-start(f32[2,32,4,34,16]{1,4,3,2,0:T(8,128)} %copy-done) | copy-start | bytes 1671172
  14.1 9.1 %slice-start = ((f32[2,32,4,34,16]{1,4,3,2,0:T(8,128)}), f32[2,32,2,34,16]{1,4,3,2,0:T(8,128)S(1)}, s32[]{:S(2)}) async-start(f32[2,32,4,34,16]{1,4,3,2,0:T(8,128)} %copy-done), calls=%async_computation | async-start | bytes 2228224 | tf_op jit(solution)/shard_map/slice | solution.py:43
  24.4 1.5 %copy-start.18 = (s32[32,1,512]{2,1,0:T(1,128)S(1)}, s32[32,1,512]{2,1,0:T(1,128)}, u32[]{:S(2)}) copy-start(s32[32,1,512]{2,1,0:T(1,128)} %get-tuple-element.204) | copy-start | bytes 196612
  24.4 1.5 %copy-start.17 = (s32[32,1,512]{2,1,0:T(1,128)S(1)}, s32[32,1,512]{2,1,0:T(1,128)}, u32[]{:S(2)}) copy-start(s32[32,1,512]{2,1,0:T(1,128)} %get-tuple-element.205) | copy-start | bytes 196612
  24.4 1.5 %copy-start.16 = (s32[32,1,512]{2,1,0:T(1,128)S(1)}, s32[32,1,512]{2,1,0:T(1,128)}, u32[]{:S(2)}) copy-start(s32[32,1,512]{2,1,0:T(1,128)} %get-tuple-element.181) | copy-start | bytes 196612
  24.4 1.6 %copy-start.15 = (s32[32,1,512]{2,1,0:T(1,128)S(1)}, s32[32,1,512]{2,1,0:T(1,128)}, u32[]{:S(2)}) copy-start(s32[32,1,512]{2,1,0:T(1,128)} %get-tuple-element.180) | copy-start | bytes 196612
  25.8 1.3 %collective-permute-start.2 = (f32[2,32,1,32]{1,3,0,2:T(8,128)S(1)}, f32[2,32,1,32]{1,3,0,2:T(8,128)S(1)}, u32[]{:S(2)}, u32[]{:S(2)}) collective-permute-start(f32[2,32,1,32]{1,3,0,2:T(8,128)S(1)} %bitcast.267), channel_id=1, source_target_pairs={{0,1},{1,0},{2,3},{3,2},{4,5},{5,4},{6,7},{7,6},{8,9},{9,8},{10,11... | collective-permute-start | bytes 24584 | tf_op jit(solution)/shard_map/ppermute | solution.py:17
  26.1 1.4 %collective-permute-start.3 = (f32[2,32,1,32]{1,3,0,2:T(8,128)S(1)}, f32[2,32,1,32]{1,3,0,2:T(8,128)S(1)}, u32[]{:S(2)}, u32[]{:S(2)}) collective-permute-start(f32[2,32,1,32]{1,3,0,2:T(8,128)S(1)} %bitcast.266), channel_id=1, source_target_pairs={{1,0},{0,1},{3,2},{2,3},{5,4},{4,5},{7,6},{6,7},{9,8},{8,9},{11,10... | collective-permute-start | bytes 24584 | tf_op jit(solution)/shard_map/ppermute | solution.py:18
  30.8 4.4 %copy-start.9 = (pred[1,32,2,512]{1,3,2,0:T(8,128)(4,1)S(1)}, pred[1,32,2,512]{1,3,2,0:T(8,128)(4,1)}, u32[]{:S(2)}) copy-start(pred[1,32,2,512]{1,3,2,0:T(8,128)(4,1)} %get-tuple-element.148) | copy-start | bytes 98308
  30.8 4.4 %copy-start.10 = (pred[1,32,2,512]{1,3,2,0:T(8,128)(4,1)S(1)}, pred[1,32,2,512]{1,3,2,0:T(8,128)(4,1)}, u32[]{:S(2)}) copy-start(pred[1,32,2,512]{1,3,2,0:T(8,128)(4,1)} %get-tuple-element.155) | copy-start | bytes 98308
  30.8 4.4 %copy-start.11 = (pred[1,32,2,512]{1,3,2,0:T(8,128)(4,1)S(1)}, pred[1,32,2,512]{1,3,2,0:T(8,128)(4,1)}, u32[]{:S(2)}) copy-start(pred[1,32,2,512]{1,3,2,0:T(8,128)(4,1)} %get-tuple-element.156) | copy-start | bytes 98308
  34.6 1.0 copy-start.2
  35.2 0.9 copy-start.6
  35.2 1.0 copy-start.7
  35.2 1.0 copy-start.8
  36.2 0.9 copy-start.3
  36.3 1.0 copy-start.4
  36.3 1.0 copy-start.5
  38.4 1.9 %copy-start.14 = (f32[1,32,512]{2,1,0:T(8,128)S(1)}, f32[1,32,512]{2,1,0:T(8,128)}, u32[]{:S(2)}) copy-start(f32[1,32,512]{2,1,0:T(8,128)} %get-tuple-element.192) | copy-start | bytes 196612
  40.2 12.5 %collective-permute-start.4 = (f32[2,32,1,544]{3,1,2,0:T(8,128)}, f32[2,32,1,544]{3,1,2,0:T(8,128)}, u32[]{:S(2)}, u32[]{:S(2)}) collective-permute-start(f32[2,32,1,544]{3,1,2,0:T(8,128)} %copy.106), channel_id=1, source_target_pairs={{0,2},{2,4},{4,6},{6,8},{8,10},{10,12},{12,14},{14,16},{16,18},{18... | collective-permute-start | bytes 417800 | tf_op jit(solution)/shard_map/ppermute | solution.py:17
  47.1 9.6 %collective-permute-start.5 = (f32[2,32,1,544]{3,1,2,0:T(8,128)}, f32[2,32,1,544]{3,1,2,0:T(8,128)}, u32[]{:S(2)}, u32[]{:S(2)}) collective-permute-start(f32[2,32,1,544]{3,1,2,0:T(8,128)} %copy.109), channel_id=1, source_target_pairs={{2,0},{4,2},{6,4},{8,6},{10,8},{12,10},{14,12},{16,14},{18,16},{20... | collective-permute-start | bytes 417800 | tf_op jit(solution)/shard_map/ppermute | solution.py:18
  54.6 3.5 %copy-start.19 = (f32[16]{0:T(128)S(1)}, f32[16]{0:T(128)}, u32[]{:S(2)}) copy-start(f32[16]{0:T(128)} %reduce_sum.226) | copy-start | bytes 196
  58.0 1.3 %collective-permute-start.6 = (f32[2,32,1,32]{1,3,0,2:T(8,128)S(1)}, f32[2,32,1,32]{1,3,0,2:T(8,128)S(1)}, u32[]{:S(2)}, u32[]{:S(2)}) collective-permute-start(f32[2,32,1,32]{1,3,0,2:T(8,128)S(1)} %bitcast.269), channel_id=1, source_target_pairs={{0,1},{1,0},{2,3},{3,2},{4,5},{5,4},{6,7},{7,6},{8,9},{9,8},{10,11... | collective-permute-start | bytes 24584 | tf_op jit(solution)/shard_map/ppermute | solution.py:17
  58.2 1.4 %collective-permute-start.7 = (f32[2,32,1,32]{1,3,0,2:T(8,128)S(1)}, f32[2,32,1,32]{1,3,0,2:T(8,128)S(1)}, u32[]{:S(2)}, u32[]{:S(2)}) collective-permute-start(f32[2,32,1,32]{1,3,0,2:T(8,128)S(1)} %bitcast.268), channel_id=1, source_target_pairs={{1,0},{0,1},{3,2},{2,3},{5,4},{4,5},{7,6},{6,7},{9,8},{8,9},{11,10... | collective-permute-start | bytes 24584 | tf_op jit(solution)/shard_map/ppermute | solution.py:18
where the time goes:
time: 108 us
  blocking collectives  40.4 us (37%)
  local copies, waits for them, and re-layouts  25.6 us (24%)
  other arithmetic  23.8 us (22%)
  starting transfers between devices  13.8 us (13%)
  waiting for transfers between devices  2.67 us (2%)
  between operations  1.49 us (1%)
    psum x1, blocking collectives, shards(): totals.append(lax.psum(terms, ('gx', 'gy')))  40.4 us
    ppermute x4, starting transfers between devices, padded(): after = lax.ppermute(leading, axis, down)  10.7 us
    unnamed x48, local copies, waits for them, and re-layouts  3.88 us
    ppermute x2, local copies, waits for them, and re-layouts, padded(): before = lax.ppermute(last, axis, up)  3.87 us
    slice x4, local copies, waits for them, and re-layouts, padded(): leading = lax.slice_in_dim(array, 0, width, axis=dim)  3.72 us
    eq x2, other arithmetic, spread(): chosen = jnp.where((codes == direction)[None], state, jnp.zeros_like(state))  3.36 us
    ppermute x4, starting transfers between devices, padded(): before = lax.ppermute(last, axis, up)  3.11 us
    scatter-add x4, other arithmetic, settle(): middle = extended[:, :, 1:cols + 1].at[:, :, 0].add(got[:, :, 0]).at[:, :...  2.53 us
  transfers between devices with their start and end apart: 8, of which 5 were waited for; matrix products, arithmetic and copies ran while one was open for 20% of the time, Pallas kernels for 0%

commit v1 on v0

--- a/solution.py
+++ b/solution.py
@@ -2,6 +2,7 @@
 import jax.numpy as jnp
 from jax import lax
 from jax.sharding import PartitionSpec as P
+from jax.lax import psum
 
 LEVELS = 16
 count_unit = 4096.0
@@ -125,7 +126,11 @@
         count_sum = jnp.sum(state[0], axis=(0, 1, 2))
         liquid_sum = jnp.sum(state[0] * state[1], axis=(0, 1, 2))
         terms = jnp.stack([count_sum, liquid_sum])
-        totals.append(lax.psum(terms, ("gx", "gy")))
+
+        def panel_view(sample, named_axis, shard_axis):
+            return psum(psum(sample, named_axis), shard_axis)
+
+        totals.append(panel_view(terms, "gy", "gx"))
     summed = jnp.stack(totals)
     cells_x = cols * lax.axis_size("gx")
     cells_y = rows * lax.axis_size("gy")

time: 108 us -> 113 us (1.046)
  blocking collectives: 40.4 us -> 45.1 us
    psum x1 -> x2, blocking collectives: 40.4 us -> 45.1 us  [panel_view(): return psum(psum(sample, named_axis), shard_axis)]
  transfers between devices with their start and end apart: 8 -> 8, of which waited for: 5 -> 5; matrix products, arithmetic and copies ran while one was open for 20% -> 19% of each run, Pallas kernels for 0% -> 0%
where the time goes in v1:
time: 113 us; the launch traced here: 112 us
  blocking collectives  45.1 us (40%)
  local copies, waits for them, and re-layouts  25.6 us (23%)
  other arithmetic  23.8 us (21%)
  starting transfers between devices  13.8 us (12%)
  waiting for transfers between devices  2.67 us (2%)
  between operations  1.49 us (1%)
    psum x2, blocking collectives, panel_view(): return psum(psum(sample, named_axis), shard_axis)  45.1 us
    ppermute x4, starting transfers between devices, padded(): after = lax.ppermute(leading, axis, down)  10.7 us
    unnamed x48, local copies, waits for them, and re-layouts  3.88 us
    ppermute x2, local copies, waits for them, and re-layouts, padded(): before = lax.ppermute(last, axis, up)  3.87 us
    slice x4, local copies, waits for them, and re-layouts, padded(): leading = lax.slice_in_dim(array, 0, width, axis=dim)  3.72 us
    eq x2, other arithmetic, spread(): chosen = jnp.where((codes == direction)[None], state, jnp.zeros_like(state))  3.36 us
    ppermute x4, starting transfers between devices, padded(): before = lax.ppermute(last, axis, up)  3.11 us
    scatter-add x4, other arithmetic, settle(): middle = extended[:, :, 1:cols + 1].at[:, :, 0].add(got[:, :, 0]).at[:, :...  2.53 us
  transfers between devices with their start and end apart: 8, of which 5 were waited for; matrix products, arithmetic and copies ran while one was open for 19% of the time, Pallas kernels for 0%

profile of v1, /device:TPU:0, one launch (start us, length us, event | category | flops | bytes accessed | tf_op | source)
XLA Modules:
  0.0 112.4 jit_solution(3750869834975199675)
XLA Ops:
  0.6 1.0 fusion.55
  1.9 0.8 broadcast_compare_fusion.16
  3.1 1.2 %broadcast_select_fusion.17 = (f32[2,32,2,32,16]{1,4,3,2,0:T(8,128)S(1)}, f32[2,32,2,32,16]{1,4,3,2,0:T(8,128)S(1)}, f32[2,32,2,32,16]{1,4,3,2,0:T(8,128)S(1)}, ...) fusion(f32[2,32,2,32,16]{1,4,3,2,0:T(8,128)S(1)} %bitcast.217, ...), kind=kLoop, calls=%fused_computation.50 | loop fusion | flops 589824 | bytes 2916352 | tf_op jit(solution)/shard_map/jit(_where)/select_n | solution.py:30
  4.3 0.6 pad_add_fusion.1
  5.2 1.1 copy.85
  6.3 3.0 %collective-permute-start = (f32[2,32,1,544]{3,1,2,0:T(8,128)}, f32[2,32,1,544]{3,1,2,0:T(8,128)}, u32[]{:S(2)}, u32[]{:S(2)}) collective-permute-start(f32[2,32,1,544]{3,1,2,0:T(8,128)} %copy.85), channel_id=1, source_target_pairs={{0,2},{2,4},{4,6},{6,8},{8,10},{10,12},{12,14},{14,16},{16,18},{18... | collective-permute-start | bytes 417800 | tf_op jit(solution)/shard_map/ppermute | solution.py:18
  9.2 0.9 copy.88
  10.1 4.0 %collective-permute-start.1 = (f32[2,32,1,544]{3,1,2,0:T(8,128)}, f32[2,32,1,544]{3,1,2,0:T(8,128)}, u32[]{:S(2)}, u32[]{:S(2)}) collective-permute-start(f32[2,32,1,544]{3,1,2,0:T(8,128)} %copy.88), channel_id=1, source_target_pairs={{2,0},{4,2},{6,4},{8,6},{10,8},{12,10},{14,12},{16,14},{18,16},{20... | collective-permute-start | bytes 417800 | tf_op jit(solution)/shard_map/ppermute | solution.py:19
  14.1 0.7 slice_bitcast_fusion.5
  14.8 1.0 copy.130
  15.9 2.5 %broadcast_compare_fusion.17 = (pred[1,32,2,512]{1,3,2,0:T(8,128)(4,1)}, pred[1,32,2,512]{1,3,2,0:T(8,128)(4,1)}, pred[1,32,2,512]{1,3,2,0:T(8,128)(4,1)}, pred[...) fusion(s32[1,32,2,512]{1,3,2,0:T(8,128)} %copy.130), kind=kLoop, calls=%fused_computation.87 | loop fusion | flops 294912 | bytes 425984 | tf_op jit(solution)/shard_map/eq | solution.py:30
  18.4 2.0 %fusion.56 = (s32[32,1,512]{2,1,0:T(1,128)}, s32[32,1,512]{2,1,0:T(1,128)}, s32[32,1,512]{2,1,0:T(1,128)}, s32[32,1,512]{2,1,0:T(1,128)}) fusion(s32[32,2,512]{2,1,0:T(2,128)} %get-tuple-element.168, s32[32,2,512]{2,1,0:T(2,128)} %get-tuple-element.169), kind=kLoop, calls=%fused_computation.232 | loop fusion | bytes 524288 | tf_op jit(solution)/shard_map/slice | solution.py:110
  20.4 0.9 fusion.57
  21.3 1.9 %copy.86 = f32[2,32,1,544]{1,3,0,2:T(8,128)} copy(f32[2,32,1,544]{3,1,2,0:T(8,128)} %collective-permute-done) | data formatting | bytes 278528 | tf_op jit(solution)/shard_map/ppermute | solution.py:18
  23.3 1.1 %fusion.3 = f32[2,32,2,34,16]{1,4,3,2,0:T(8,128)S(1)} fusion(f32[2,32,2,34,16]{1,4,3,2,0:T(8,128)S(1)} %slice-done, f32[2,32,1,34,16]{1,4,3,2,0:T(8,128)} %bitcast.218, f32[2,32,4,34,16]{1,4,3,2,0:T(8,128)S(1)} %copy-done.1), kind=kLoop, calls=%fused_computation.32 | loop fusion | flops 34816 | bytes 1253376 | tf_op jit(solution)/shard_map/scatter-add | solution.py:46
  24.4 1.2 %copy.89 = f32[2,32,1,544]{1,3,0,2:T(8,128)S(1)} copy(f32[2,32,1,544]{3,1,2,0:T(8,128)} %collective-permute-done.1) | data formatting | bytes 278528 | tf_op jit(solution)/shard_map/ppermute | solution.py:19
  26.1 0.6 collective-permute-start.3
  26.7 0.4 collective-permute-done.2
  27.1 0.5 collective-permute-done.3
  27.7 0.4 select_reduce_fusion.11
  28.3 0.4 select_reduce_fusion.15
  28.9 0.4 select_reduce_fusion.9
  29.4 0.4 select_reduce_fusion.13
  29.9 0.8 select_bitcast_fusion.7
  30.8 0.4 select_reduce_fusion.14
  31.2 0.6 convert_bitcast_fusion.3
  31.8 0.7 fusion.15
  32.7 0.4 select_reduce_fusion.12
  33.2 0.4 select_reduce_fusion.10
  33.5 0.6 convert_bitcast_fusion.2
  34.3 0.4 select_reduce_fusion.8
  35.6 0.5 copy-done.6
  36.6 0.5 copy-done.3
  37.6 0.6 pad_add_fusion
  38.5 0.9 fusion.52
  39.3 0.9 copy.106
  40.3 0.9 maximum_bitcast_fusion.3
  41.2 0.6 fusion.48
  41.8 0.8 reduce_sum.225
  42.6 1.4 %reduce_sum.228 = f32[32,16]{1,0:T(8,128)} reshape(f32[512]{0:T(512)} %get-tuple-element.105) | data formatting | bytes 4096 | tf_op jit(solution)/shard_map/reduce_sum | solution.py:127
  43.9 0.5 reduce_sum.226
  44.5 0.7 reduce_sum.229
  45.2 1.9 %copy.109 = f32[2,32,1,544]{3,1,2,0:T(8,128)} copy(f32[2,32,1,544]{1,3,2,0:T(8,128)} %get-tuple-element.118) | data formatting | bytes 278528 | tf_op jit(solution)/shard_map/slice | solution.py:17
  47.1 5.6 %collective-permute-start.5 = (f32[2,32,1,544]{3,1,2,0:T(8,128)}, f32[2,32,1,544]{3,1,2,0:T(8,128)}, u32[]{:S(2)}, u32[]{:S(2)}) collective-permute-start(f32[2,32,1,544]{3,1,2,0:T(8,128)} %copy.109), channel_id=1, source_target_pairs={{2,0},{4,2},{6,4},{8,6},{10,8},{12,10},{14,12},{16,14},{18,16},{20... | collective-permute-start | bytes 417800 | tf_op jit(solution)/shard_map/ppermute | solution.py:19
  52.7 1.9 %copy.107 = f32[2,32,1,544]{1,3,0,2:T(8,128)} copy(f32[2,32,1,544]{3,1,2,0:T(8,128)} %collective-permute-done.4) | data formatting | bytes 278528 | tf_op jit(solution)/shard_map/ppermute | solution.py:18
  54.6 1.1 %fusion.1 = f32[2,32,2,34,16]{1,4,3,2,0:T(8,128)S(1)} fusion(f32[2,32,2,34,16]{1,4,3,2,0:T(8,128)S(1)} %slice.539, f32[2,32,1,34,16]{1,4,3,2,0:T(8,128)} %bitcast.219, f32[2,32,4,34,16]{1,4,3,2,0:T(8,128)S(1)} %pad_add_fusion), kind=kLoop, calls=%fused_computation.28 | loop fusion | flops 34816 | bytes 1253376 | tf_op jit(solution)/shard_map/scatter-add | solution.py:46
  55.8 1.0 collective-permute-done.5
  56.7 1.1 copy.110
  58.2 0.5 collective-permute-start.7
  58.8 0.5 collective-permute-done.6
  59.8 0.4 select_reduce_fusion.3
  60.4 0.4 select_reduce_fusion.7
  61.0 0.4 select_reduce_fusion.1
  61.6 0.4 select_reduce_fusion.5
  62.0 0.8 select_bitcast_fusion.3
  62.9 0.4 select_reduce_fusion.6
  63.3 0.7 fusion.19
  64.2 0.4 select_reduce_fusion.4
  64.7 0.4 select_reduce_fusion.2
  65.2 0.4 select_reduce_fusion
  65.8 0.9 copy.125
  66.8 2.5 %all-reduce.19 = (f32[2,16]{1,0:T(2,128)S(1)}, f32[2,16]{1,0:T(2,128)S(1)}) all-reduce(f32[2,16]{1,0:T(2,128)S(1)} %pad_maximum_fusion.9, f32[2,16]{1,0:T(2,128)S(1)} %pad_maximum_fusion.8), channel_id=1, replica_groups=mesh['gx'=16,'gy'=2] {'gy'}, use_global_device_ids=true, to_apply=%region_26.27 | all-reduce | flops 64 | bytes 512 | tf_op jit(solution)/shard_map/psum | solution.py:131
  69.2 42.6 %all-reduce.18 = (f32[1,2,16]{2,1,0:T(2,128)S(1)}, f32[1,2,16]{2,1,0:T(2,128)S(1)}) all-reduce(f32[1,2,16]{2,1,0:T(2,128)S(1)} %bitcast.272, f32[1,2,16]{2,1,0:T(2,128)S(1)} %bitcast.273), channel_id=1, replica_groups=mesh['gx'=16,'gy'=2] {'gx'}, use_global_device_ids=true, to_apply=%region_27.28 | all-reduce | flops 64 | bytes 512 | tf_op jit(solution)/shard_map/psum | solution.py:131
  111.8 0.6 maximum_multiply_fusion
  (140 shorter events, 6.4 us)
Async XLA Ops:
  0.6 2.1 %copy-start.12 = (f32[2,32,2,512]{3,2,1,0:T(2,128)S(1)}, f32[2,32,2,512]{3,2,1,0:T(2,128)}, u32[]{:S(2)}) copy-start(f32[2,32,2,512]{3,2,1,0:T(2,128)} %param.20) | copy-start | bytes 786436
  4.9 9.2 %copy-start = (f32[2,32,4,34,16]{1,4,3,2,0:T(8,128)}, f32[2,32,4,34,16]{1,4,3,2,0:T(8,128)S(1)}, u32[]{:S(2)}) copy-start(f32[2,32,4,34,16]{1,4,3,2,0:T(8,128)S(1)} %pad_add_fusion.1) | copy-start | bytes 1671172
  6.3 15.0 %collective-permute-start = (f32[2,32,1,544]{3,1,2,0:T(8,128)}, f32[2,32,1,544]{3,1,2,0:T(8,128)}, u32[]{:S(2)}, u32[]{:S(2)}) collective-permute-start(f32[2,32,1,544]{3,1,2,0:T(8,128)} %copy.85), channel_id=1, source_target_pairs={{0,2},{2,4},{4,6},{6,8},{8,10},{10,12},{12,14},{14,16},{16,18},{18... | collective-permute-start | bytes 417800 | tf_op jit(solution)/shard_map/ppermute | solution.py:18
  10.1 4.0 %copy-start.13 = (s32[2,32,2,512]{3,2,1,0:T(2,128)S(1)}, s32[2,32,2,512]{3,2,1,0:T(2,128)}, u32[]{:S(2)}) copy-start(s32[2,32,2,512]{3,2,1,0:T(2,128)} %param.22) | copy-start | bytes 786436
  10.1 14.3 %collective-permute-start.1 = (f32[2,32,1,544]{3,1,2,0:T(8,128)}, f32[2,32,1,544]{3,1,2,0:T(8,128)}, u32[]{:S(2)}, u32[]{:S(2)}) collective-permute-start(f32[2,32,1,544]{3,1,2,0:T(8,128)} %copy.88), channel_id=1, source_target_pairs={{2,0},{4,2},{6,4},{8,6},{10,8},{12,10},{14,12},{16,14},{18,16},{20... | collective-permute-start | bytes 417800 | tf_op jit(solution)/shard_map/ppermute | solution.py:19
  14.1 9.1 %copy-start.1 = (f32[2,32,4,34,16]{1,4,3,2,0:T(8,128)S(1)}, f32[2,32,4,34,16]{1,4,3,2,0:T(8,128)}, u32[]{:S(2)}) copy-start(f32[2,32,4,34,16]{1,4,3,2,0:T(8,128)} %copy-done) | copy-start | bytes 1671172
  14.1 9.1 %slice-start = ((f32[2,32,4,34,16]{1,4,3,2,0:T(8,128)}), f32[2,32,2,34,16]{1,4,3,2,0:T(8,128)S(1)}, s32[]{:S(2)}) async-start(f32[2,32,4,34,16]{1,4,3,2,0:T(8,128)} %copy-done), calls=%async_computation | async-start | bytes 2228224 | tf_op jit(solution)/shard_map/slice | solution.py:44
  24.4 1.5 %copy-start.18 = (s32[32,1,512]{2,1,0:T(1,128)S(1)}, s32[32,1,512]{2,1,0:T(1,128)}, u32[]{:S(2)}) copy-start(s32[32,1,512]{2,1,0:T(1,128)} %get-tuple-element.206) | copy-start | bytes 196612
  24.4 1.5 %copy-start.17 = (s32[32,1,512]{2,1,0:T(1,128)S(1)}, s32[32,1,512]{2,1,0:T(1,128)}, u32[]{:S(2)}) copy-start(s32[32,1,512]{2,1,0:T(1,128)} %get-tuple-element.207) | copy-start | bytes 196612
  24.4 1.5 %copy-start.16 = (s32[32,1,512]{2,1,0:T(1,128)S(1)}, s32[32,1,512]{2,1,0:T(1,128)}, u32[]{:S(2)}) copy-start(s32[32,1,512]{2,1,0:T(1,128)} %get-tuple-element.183) | copy-start | bytes 196612
  24.4 1.6 %copy-start.15 = (s32[32,1,512]{2,1,0:T(1,128)S(1)}, s32[32,1,512]{2,1,0:T(1,128)}, u32[]{:S(2)}) copy-start(s32[32,1,512]{2,1,0:T(1,128)} %get-tuple-element.182) | copy-start | bytes 196612
  25.8 1.3 %collective-permute-start.2 = (f32[2,32,1,32]{1,3,0,2:T(8,128)S(1)}, f32[2,32,1,32]{1,3,0,2:T(8,128)S(1)}, u32[]{:S(2)}, u32[]{:S(2)}) collective-permute-start(f32[2,32,1,32]{1,3,0,2:T(8,128)S(1)} %bitcast.265), channel_id=1, source_target_pairs={{0,1},{1,0},{2,3},{3,2},{4,5},{5,4},{6,7},{7,6},{8,9},{9,8},{10,11... | collective-permute-start | bytes 24584 | tf_op jit(solution)/shard_map/ppermute | solution.py:18
  26.1 1.4 %collective-permute-start.3 = (f32[2,32,1,32]{1,3,0,2:T(8,128)S(1)}, f32[2,32,1,32]{1,3,0,2:T(8,128)S(1)}, u32[]{:S(2)}, u32[]{:S(2)}) collective-permute-start(f32[2,32,1,32]{1,3,0,2:T(8,128)S(1)} %bitcast.264), channel_id=1, source_target_pairs={{1,0},{0,1},{3,2},{2,3},{5,4},{4,5},{7,6},{6,7},{9,8},{8,9},{11,10... | collective-permute-start | bytes 24584 | tf_op jit(solution)/shard_map/ppermute | solution.py:19
  30.8 4.4 %copy-start.9 = (pred[1,32,2,512]{1,3,2,0:T(8,128)(4,1)S(1)}, pred[1,32,2,512]{1,3,2,0:T(8,128)(4,1)}, u32[]{:S(2)}) copy-start(pred[1,32,2,512]{1,3,2,0:T(8,128)(4,1)} %get-tuple-element.150) | copy-start | bytes 98308
  30.8 4.4 %copy-start.10 = (pred[1,32,2,512]{1,3,2,0:T(8,128)(4,1)S(1)}, pred[1,32,2,512]{1,3,2,0:T(8,128)(4,1)}, u32[]{:S(2)}) copy-start(pred[1,32,2,512]{1,3,2,0:T(8,128)(4,1)} %get-tuple-element.157) | copy-start | bytes 98308
  30.8 4.4 %copy-start.11 = (pred[1,32,2,512]{1,3,2,0:T(8,128)(4,1)S(1)}, pred[1,32,2,512]{1,3,2,0:T(8,128)(4,1)}, u32[]{:S(2)}) copy-start(pred[1,32,2,512]{1,3,2,0:T(8,128)(4,1)} %get-tuple-element.158) | copy-start | bytes 98308
  34.6 1.0 copy-start.2
  35.2 0.9 copy-start.6
  35.2 1.0 copy-start.7
  35.2 1.0 copy-start.8
  36.2 0.9 copy-start.3
  36.3 1.0 copy-start.4
  36.3 1.0 copy-start.5
  38.4 1.9 %copy-start.14 = (f32[1,32,512]{2,1,0:T(8,128)S(1)}, f32[1,32,512]{2,1,0:T(8,128)}, u32[]{:S(2)}) copy-start(f32[1,32,512]{2,1,0:T(8,128)} %get-tuple-element.194) | copy-start | bytes 196612
  40.2 12.5 %collective-permute-start.4 = (f32[2,32,1,544]{3,1,2,0:T(8,128)}, f32[2,32,1,544]{3,1,2,0:T(8,128)}, u32[]{:S(2)}, u32[]{:S(2)}) collective-permute-start(f32[2,32,1,544]{3,1,2,0:T(8,128)} %copy.106), channel_id=1, source_target_pairs={{0,2},{2,4},{4,6},{6,8},{8,10},{10,12},{12,14},{14,16},{16,18},{18... | collective-permute-start | bytes 417800 | tf_op jit(solution)/shard_map/ppermute | solution.py:18
  47.1 9.6 %collective-permute-start.5 = (f32[2,32,1,544]{3,1,2,0:T(8,128)}, f32[2,32,1,544]{3,1,2,0:T(8,128)}, u32[]{:S(2)}, u32[]{:S(2)}) collective-permute-start(f32[2,32,1,544]{3,1,2,0:T(8,128)} %copy.109), channel_id=1, source_target_pairs={{2,0},{4,2},{6,4},{8,6},{10,8},{12,10},{14,12},{16,14},{18,16},{20... | collective-permute-start | bytes 417800 | tf_op jit(solution)/shard_map/ppermute | solution.py:19
  54.6 3.5 %copy-start.19 = (f32[16]{0:T(128)S(1)}, f32[16]{0:T(128)}, u32[]{:S(2)}) copy-start(f32[16]{0:T(128)} %reduce_sum.226) | copy-start | bytes 196
  58.0 1.3 %collective-permute-start.6 = (f32[2,32,1,32]{1,3,0,2:T(8,128)S(1)}, f32[2,32,1,32]{1,3,0,2:T(8,128)S(1)}, u32[]{:S(2)}, u32[]{:S(2)}) collective-permute-start(f32[2,32,1,32]{1,3,0,2:T(8,128)S(1)} %bitcast.267), channel_id=1, source_target_pairs={{0,1},{1,0},{2,3},{3,2},{4,5},{5,4},{6,7},{7,6},{8,9},{9,8},{10,11... | collective-permute-start | bytes 24584 | tf_op jit(solution)/shard_map/ppermute | solution.py:18
  58.2 1.4 %collective-permute-start.7 = (f32[2,32,1,32]{1,3,0,2:T(8,128)S(1)}, f32[2,32,1,32]{1,3,0,2:T(8,128)S(1)}, u32[]{:S(2)}, u32[]{:S(2)}) collective-permute-start(f32[2,32,1,32]{1,3,0,2:T(8,128)S(1)} %bitcast.266), channel_id=1, source_target_pairs={{1,0},{0,1},{3,2},{2,3},{5,4},{4,5},{7,6},{6,7},{9,8},{8,9},{11,10... | collective-permute-start | bytes 24584 | tf_op jit(solution)/shard_map/ppermute | solution.py:19
